TPU v7x, 32 devices: a whole 2x2x4 slice. The times are simulated.
32 devices in a mesh: gx: 4 (over z), gy: 2 (over y), gz: 4 (over x, core).
Axes of the slice: x: 2, y: 2, z: 4, core: 2. Of those that a mesh axis runs over, the one named last changes fastest.
Arguments:
- positions: float32 [3, 8, 4, 32, 128], P(None, 'gx', 'gy', 'gz'), may hold values from 0 to 1
- shield: float32 [8, 4, 32, 128], P('gx', 'gy', 'gz'), may hold values from 0.3 to 1
- width: float32 [8, 4, 32, 128], P('gx', 'gy', 'gz'), may hold values from 0.5 to 2
- hardness: float32 [8, 4, 32, 128], P('gx', 'gy', 'gz'), may hold values from 0.5 to 2
- softness: float32 [8, 4, 32, 128], P('gx', 'gy', 'gz'), may hold values from 0.5 to 2
- coupling: float32 [8, 4, 32, 128], P('gx', 'gy', 'gz'), may hold values from -0.45 to 0.45
- pair_bits: int32 [8, 4, 32], P('gx', 'gy', 'gz'), may hold values from 8192 to 134217727
- right_side: float32 [4, 8, 4, 32, 128], P(None, 'gx', 'gy', 'gz'), may hold values from -7 to 7
Outputs:
- solution: float32 [4, 8, 4, 32, 128], P(None, 'gx', 'gy', 'gz')
- residual: float32 [4, 8, 4, 32, 128], P(None, 'gx', 'gy', 'gz')
All inputs are finite; a program needn't handle non-finite values.
Results may differ from a plain program's by a relative error of at most 0.0018.
Values sent between devices are 32-bit elements; how exact they have to be, the bound alone decides.
A program may use at most 128 MiB of HBM per device.

v0:
```python
import functools
import itertools

import jax
import jax.numpy as jnp
from jax import lax
from jax.experimental import pallas as pl
from jax.experimental.pallas import tpu as pltpu
from jax.sharding import PartitionSpec as P

ITERS = 3
AXES = ("gx", "gy", "gz")
DIRECTIONS = [d for d in itertools.product((-1, 0, 1), repeat=3) if d != (0, 0, 0)]

coulomb_scale = 0.002
response_scale = 0.003


def sides(step, count, unit):
    if step < 0:
        return pl.ds(unit, unit), pl.ds((count + 1) * unit, unit)
    if step > 0:
        return pl.ds(count * unit, unit), pl.ds(0, unit)
    return pl.ds(unit, count * unit), pl.ds(unit, count * unit)


def kernel(
    counts, extent, tile,
    bits_ref, params_ref, rhs_ref, aux_ref, sol_ref, res_ref,
    store, param_pad, rem_pad, along_pad, ghosts, lhs, columns, diag, direction, sums, parts,
    halo_send, halo_recv, sum_send, sum_recv,
):
    tx, ty, tz = extent
    me = [lax.axis_index(axis) for axis in AXES]

    def exists(d):
        ok = None
        for m, step, count in zip(me, d, counts):
            if step:
                here = (m + step >= 0) & (m + step < count)
                ok = here if ok is None else ok & here
        return ok

    def halo_copy(ref, slot, index, d):
        pairs = [sides(s, n, u) for s, n, u in zip(d, extent, (1, 1, tile))]
        source = (pairs[0][0], pairs[1][0], slice(None), pairs[2][0])
        target = (pairs[0][1], pairs[1][1], slice(None), pairs[2][1])
        return pltpu.make_async_remote_copy(
            src_ref=ref.at[source],
            dst_ref=ref.at[target],
            send_sem=halo_send.at[slot, index],
            recv_sem=halo_recv.at[slot, index],
            device_id=tuple(m + s for m, s in zip(me, d)),
            device_id_type=pl.DeviceIdType.MESH,
        )

    def halo_start(ref, slot, fill):
        for index, d in enumerate(DIRECTIONS):
            there = exists(d)

            @pl.when(there)
            def _():
                halo_copy(ref, slot, index, d).start()

            back = tuple(-s for s in d)
            strips = [sides(s, n, u)[1] for s, n, u in zip(back, extent, (1, 1, tile))]

            @pl.when(jnp.logical_not(there))
            def _():
                region = (strips[0], strips[1], slice(None), strips[2])
                ref[region] = jnp.full(ref.at[region].shape, fill, jnp.float32)

    def halo_wait(ref, slot):
        for index, d in enumerate(DIRECTIONS):
            @pl.when(exists(d))
            def _():
                halo_copy(ref, slot, index, d).wait_send()

            back = tuple(-s for s in d)

            @pl.when(exists(back))
            def _():
                halo_copy(ref, slot, index, d).wait_recv()

    rank = (me[0] * counts[1] + me[1]) * counts[2] + me[2]
    hops = [h for h in itertools.product(*map(range, counts)) if any(h)]

    def reduced(slot, value):
        sums[slot] = value
        parts[slot, rank] = value
        copies = [
            pltpu.make_async_remote_copy(
                src_ref=sums.at[slot],
                dst_ref=parts.at[slot, rank],
                send_sem=sum_send.at[slot, j],
                recv_sem=sum_recv.at[slot, j],
                device_id=tuple(lax.rem(m + h, n) for m, h, n in zip(me, hop, counts)),
                device_id_type=pl.DeviceIdType.MESH,
            )
            for j, hop in enumerate(hops)
        ]
        for copy in copies:
            copy.start()
        for copy in copies:
            copy.wait()
        value = jnp.sum(parts[slot], axis=0)
        total = jnp.sum(value, axis=1, keepdims=True)
        norm, product = total[:4], total[4:]

        def both(x):
            return x + jnp.concatenate([x[2:4], x[0:2]], axis=0)

        return both(norm), both(product)

    inside = pl.ds(tile, tz * tile)
    for a in range(tx):
        for b in range(ty):
            param_pad[a + 1, b + 1, :, inside] = params_ref[a, b]
            rem_pad[a + 1, b + 1, :, inside] = rhs_ref[a, b]
    halo_start(param_pad, 0, 1.0)
    halo_start(rem_pad, 1, 0.0)

    row = lax.broadcasted_iota(jnp.int32, (8, tile), 0)

    def centred(value):
        return jnp.where(row < 3, value - 0.5, value)

    def squares(value):
        return value[0:1] * value[0:1] + value[1:2] * value[1:2] + value[2:3] * value[2:3]

    def three(value):
        first = value.astype(jnp.bfloat16).astype(jnp.float32)
        rest = value - first
        second = rest.astype(jnp.bfloat16).astype(jnp.float32)
        return first, second, rest - second

    def source_block(ap, bp, p, widths):
        start = pl.multiple_of(p * tile, tile)
        raw = param_pad[ap, bp, :, pl.ds(start, tile)]
        x = centred(raw)
        x = jnp.where(row == 4, 0.0, jnp.where(row == 5, squares(x), x))
        x = jnp.where(row == 7, 0.0, x)
        x1, x2, x3 = three(x)
        turned = jnp.concatenate([x1, x1, x1, x2, x2, x3, raw, raw], axis=0).T
        columns[...] = jnp.broadcast_to(turned[:, 52:53], (tile, tile)) * -0.6931471805599453
        partner = turned.astype(jnp.bfloat16)

        def visit(rows_of_tiles):
            for (a, b), c in itertools.product(rows_of_tiles, widths):
                o = (ap - 1 - a, bp - 1 - b, p - 1 - c)
                code = 9 * (o[0] + 1) + 3 * (o[1] + 1) + (o[2] + 1)
                t = (a * ty + b) * tz + c
                listed = jnp.right_shift(bits_ref[t], code) & 1
                own = param_pad[
                    a + 1, b + 1, :, pl.ds(pl.multiple_of((c + 1) * tile, tile), tile)
                ]
                shift = [step.astype(jnp.float32) for step in o]
                shift = jnp.where(row == 0, shift[0], jnp.where(row == 1, shift[1], shift[2]))
                r = centred(own) - shift
                y = jnp.where(row < 3, -2.0 * r, jnp.where(row == 6, squares(r), own))
                y = jnp.where((row == 4) | (row == 7), 0.0, y)
                blank = jnp.zeros((16, tile), jnp.float32)
                halves = []
                for half in (jnp.where(row == 3, 0.0, y), y):
                    y1, y2, y3 = three(half)
                    halves.append(jnp.concatenate([y1, y2, y3, y1, y2, y1, blank], axis=0))
                factors = jnp.concatenate(halves, axis=1).astype(jnp.bfloat16)
                got = jnp.dot(partner, factors, preferred_element_type=jnp.float32)
                listed = listed.astype(jnp.float32)
                coulomb = lax.rsqrt(got[:, tile:]) * (coulomb_scale * listed)
                span = columns[...] + own[4:5] * -0.6931471805599453
                response = jnp.exp2(got[:, :tile] / span) * (response_scale * listed)
                rows = pl.ds(pl.multiple_of(code * tile, tile), tile)
                store[t, rows, 0:tile] = coulomb.astype(jnp.bfloat16)
                store[t, rows, tile : 2 * tile] = response.astype(jnp.bfloat16)

        a_low, b_low = jnp.maximum(ap - 2, 0), jnp.maximum(bp - 2, 0)
        wide = jnp.minimum(bp, ty - 1) + 1 - b_low
        total = (jnp.minimum(ap, tx - 1) + 1 - a_low) * wide

        def place(n):
            return a_low + n // wide, b_low + n % wide

        def two(n, carry):
            visit([place(2 * n), place(2 * n + 1)])
            return carry

        def single(n, carry):
            visit([place(total - 1)])
            return carry

        lax.fori_loop(0, total // 2, two, 0)
        lax.fori_loop(0, total % 2, single, 0)

    def edge_sources(ap, bp, first, second, wide):
        def step(s, carry):
            p = first + s * (second - first)
            base = s * (tz - wide)
            source_block(ap, bp, p, [base + w for w in range(wide)])
            return carry

        lax.fori_loop(0, 2, step, 0)

    def middle_sources(ap, bp):
        def step(p, carry):
            source_block(ap, bp, p, [p - 2, p - 1, p])
            return carry

        lax.fori_loop(2, tz, step, 0)

    def own_rows(body):
        def over(q, carry):
            body(1 + q // ty, 1 + q % ty)
            return carry

        lax.fori_loop(0, tx * ty, over, 0)

    def build_own(ap, bp):
        middle_sources(ap, bp)
        edge_sources(ap, bp, 1, tz, 2)

    own_rows(build_own)

    same = lax.broadcasted_iota(jnp.int32, (tile, 2 * tile), 0) == (
        lax.broadcasted_iota(jnp.int32, (tile, 2 * tile), 1) % tile
    )

    def clear(t, carry):
        rows = pl.ds(13 * tile, tile)
        block = store[t, rows, :].astype(jnp.float32)
        store[t, rows, :] = jnp.where(same, 0.0, block).astype(jnp.bfloat16)
        return carry

    lax.fori_loop(0, tx * ty * tz, clear, 0)

    halo_wait(param_pad, 0)

    own_rows(lambda ap, bp: edge_sources(ap, bp, 0, tz + 1, 1))

    def ghost_row(q, carry):
        ap = q // (ty + 2)
        bp = q % (ty + 2)
        own = (ap >= 1) & (ap <= tx) & (bp >= 1) & (bp <= ty)
        held = (ap + me[0] >= 1) & (ap + me[0] <= tx + counts[0] - 1)
        held = held & (bp + me[1] >= 1) & (bp + me[1] <= ty + counts[1] - 1)

        @pl.when(jnp.logical_not(own) & held)
        def _():
            middle_sources(ap, bp)
            edge_sources(ap, bp, 1, tz, 2)
            edge_sources(ap, bp, 0, tz + 1, 1)

        @pl.when(jnp.logical_not(own) & jnp.logical_not(held))
        def _():
            def over_a(a, inner):
                def over_b(b, innermost):
                    code = 9 * (ap - a) + 3 * (bp - b)
                    rows = pl.ds(pl.multiple_of(code * tile, tile), 3 * tile)

                    def over_c(c, last):
                        store[(a * ty + b) * tz + c, rows, :] = jnp.zeros(
                            (3 * tile, 2 * tile), jnp.bfloat16
                        )
                        return last

                    return lax.fori_loop(0, tz, over_c, innermost)

                return lax.fori_loop(
                    jnp.maximum(bp - 2, 0), jnp.minimum(bp, ty - 1) + 1, over_b, inner
                )

            lax.fori_loop(jnp.maximum(ap - 2, 0), jnp.minimum(ap, tx - 1) + 1, over_a, 0)

        return carry

    lax.fori_loop(0, (tx + 2) * (ty + 2), ghost_row, 0)
    halo_wait(rem_pad, 1)

    charge_rows = lax.broadcasted_iota(jnp.int32, (4, tile), 0) < 2

    def operate(out, first):
        def split(q, carry):
            ap = q // (ty + 2)
            bp = q % (ty + 2)
            value = rem_pad[ap, bp]
            upper = value.astype(jnp.bfloat16).astype(jnp.float32)
            lower = value - upper
            ones = jnp.ones((8, value.shape[1]), jnp.float32)
            lhs[ap, bp] = jnp.concatenate([upper, lower, ones], axis=0).astype(jnp.bfloat16)
            return carry

        lax.fori_loop(0, (tx + 2) * (ty + 2), split, 0)

        def one(t, carry):
            norm, product = carry
            a = t // (ty * tz)
            b = t // tz % ty
            c = t % tz
            window = pl.ds(pl.multiple_of(c * tile, tile), 3 * tile)
            rows = jnp.concatenate(
                [lhs[a + i, b + j, :, window] for i in range(3) for j in range(3)], axis=1
            )
            got = jnp.dot(rows, store[t], preferred_element_type=jnp.float32)
            pair = got[0:4] + got[4:8]
            pair = jnp.where(charge_rows, pair[:, :tile], -pair[:, tile:])
            here = pl.ds(pl.multiple_of(c * tile, tile), tile)
            there = pl.ds(pl.multiple_of((c + 1) * tile, tile), tile)
            if first:
                row_sums = jnp.where(charge_rows, got[8:12, :tile], got[8:12, tile:])
                own = aux_ref[a, b, :, here]
                diag[a, b, :, here] = row_sums + jnp.where(charge_rows, own[0:1], own[1:2])
            vector = rem_pad[a + 1, b + 1, :, there]
            swapped = jnp.concatenate([vector[2:4], vector[0:2]], axis=0)
            link = aux_ref[a, b, 2:3, here]
            image = diag[a, b, :, here] * vector + pair + link * swapped
            out[a + 1, b + 1, :, there] = image
            return (norm + vector * vector, product + vector * image)

        zero = jnp.zeros((4, tile), jnp.float32)
        norm, product = lax.fori_loop(0, tx * ty * tz, one, (zero, zero), unroll=2)
        return jnp.concatenate([norm, product], axis=0)

    interior = (pl.ds(1, tx), pl.ds(1, ty), slice(None), inside)
    norm_now = step_size = None
    for iteration in range(ITERS):
        last = iteration + 1 == ITERS
        image = ghosts.at[iteration]
        partial = operate(image, iteration == 0)
        if not last:
            halo_start(image, 2 + iteration, 0.0)
        norm_next, product = reduced(iteration, partial)
        if not last:
            halo_wait(image, 2 + iteration)
        if iteration == 0:
            beta = None
            step_size = norm_next / product
        else:
            beta = norm_next / norm_now
            step_size = norm_next / (product - beta * norm_next / step_size)
        norm_now = norm_next
        for a in range(tx):
            for b in range(ty):
                along_dir = rem_pad[a + 1, b + 1, :, inside]
                if beta is not None:
                    along_dir = along_dir + beta * direction[a, b]
                direction[a, b] = along_dir
                moved = step_size * along_dir
                sol_ref[a, b] = moved if beta is None else sol_ref[a, b] + moved
        if last:
            for a in range(tx):
                for b in range(ty):
                    along = image[a + 1, b + 1, :, inside] + beta * along_pad[a + 1, b + 1, :, inside]
                    res_ref[a, b] = rem_pad[a + 1, b + 1, :, inside] - step_size * along
        else:
            for a in range(tx + 2):
                for b in range(ty + 2):
                    along = image[a, b]
                    if beta is not None:
                        along = along + beta * along_pad[a, b]
                    along_pad[a, b] = along
                    rem_pad[a, b] = rem_pad[a, b] - step_size * along


def on_device(counts, positions, shield, width, hardness, softness, coupling, pair_bits, right_side):
    tx, ty, tz, tile = hardness.shape
    blank = jnp.ones_like(width)

    def rows(fields):
        stacked = jnp.stack(fields, axis=2)
        return stacked.reshape(tx, ty, len(fields), tz * tile)

    params = rows([positions[0], positions[1], positions[2], shield, width, blank, blank, blank])
    aux = rows([hardness, softness, coupling, blank])
    rhs = rows([right_side[f] for f in range(4)])
    padded = (tx + 2, ty + 2)
    lanes = (tz + 2) * tile
    peers = counts[0] * counts[1] * counts[2]
    field = jax.ShapeDtypeStruct((tx, ty, 4, tz * tile), jnp.float32)
    vmem = pl.BlockSpec(memory_space=pltpu.VMEM)
    sol, res = pl.pallas_call(
        functools.partial(kernel, counts, (tx, ty, tz), tile),
        out_shape=(field, field),
        in_specs=[pl.BlockSpec(memory_space=pltpu.SMEM), vmem, vmem, vmem],
        out_specs=(vmem, vmem),
        scratch_shapes=[
            pltpu.VMEM((tx * ty * tz, 27 * tile, 2 * tile), jnp.bfloat16),
            pltpu.VMEM(padded + (8, lanes), jnp.float32),
            pltpu.VMEM(padded + (4, lanes), jnp.float32),
            pltpu.VMEM(padded + (4, lanes), jnp.float32),
            pltpu.VMEM((ITERS,) + padded + (4, lanes), jnp.float32),
            pltpu.VMEM(padded + (16, lanes), jnp.bfloat16),
            pltpu.VMEM((tile, tile), jnp.float32),
            pltpu.VMEM((tx, ty, 4, tz * tile), jnp.float32),
            pltpu.VMEM((tx, ty, 4, tz * tile), jnp.float32),
            pltpu.VMEM((ITERS, 8, tile), jnp.float32),
            pltpu.VMEM((ITERS, peers, 8, tile), jnp.float32),
            pltpu.SemaphoreType.DMA((ITERS + 1, 26)),
            pltpu.SemaphoreType.DMA((ITERS + 1, 26)),
            pltpu.SemaphoreType.DMA((ITERS, peers)),
            pltpu.SemaphoreType.DMA((ITERS, peers)),
        ],
        compiler_params=pltpu.CompilerParams(
            has_side_effects=True, vmem_limit_bytes=67043328
        ),
    )(pair_bits.reshape(-1), params, rhs, aux)

    def fields(x):
        return x.reshape(tx, ty, 4, tz, tile).transpose(2, 0, 1, 3, 4)

    return fields(sol), fields(res)


def solution(mesh):
    counts = tuple(mesh.shape[axis] for axis in AXES)
    tiles = P("gx", "gy", "gz", None)
    four = P(None, "gx", "gy", "gz", None)
    return jax.shard_map(
        functools.partial(on_device, counts),
        mesh=mesh,
        in_specs=(four, tiles, tiles, tiles, tiles, tiles, P("gx", "gy", "gz"), four),
        out_specs=(four, four),
        check_vma=False,
    )
```

profile of v0, /device:TPU:0, one launch (start us, length us, event | category | flops | bytes accessed | tf_op | source)
XLA Modules:
  0.0 142.1 jit_solution(12224495634326813300)
XLA Ops:
  0.6 0.0 copy-start.7
  0.6 0.7 copy-done.7
  1.3 0.7 reshape.43.bits_ref
  2.0 0.8 fusion.1
  2.7 0.0 copy-start.2
  2.7 0.0 copy-start.3
  2.8 0.7 copy-done.2
  3.5 0.0 copy-done.3
  3.5 0.0 copy-start
  3.5 0.8 stack.50.params_ref
  4.3 0.0 copy-done
  4.3 0.0 copy-start.4
  4.3 0.0 copy-start.5
  4.3 0.0 copy-start.6
  4.3 0.7 copy-done.4
  5.0 0.0 copy-done.5
  5.0 0.0 copy-done.6
  5.1 0.8 pad_maximum_fusion
  5.8 133.8 %shard_map.95 = (f32[2,2,4,1024]{3,2,1,0:T(4,128)}, f32[2,2,4,1024]{3,2,1,0:T(4,128)}) custom-call(s32[32]{0:T(128)} %reshape.43.bits_ref, f32[2,2,8,1024]{3,2,1,0:T(8,128)} %stack.50.params_ref, f32[2,2,4,1024]{3,2,1,0:T(4,128)} %get-tuple-element.13.rhs_ref, f32[2,2,4,1024]{3,2,1,0:T(4,128)} %get-tuple-element.14.aux_ref), custom_call_target="tpu_custom_call" | custom-call | tf_op jit(solution)/shard_map/pallas_call | solution.py:380
  139.7 0.9 reshape.44
  140.5 0.0 copy-start.1
  140.6 0.6 copy.15
  141.2 0.2 copy-done.1
  141.4 0.6 copy.14
  (4 shorter events, 0.1 us)
Async XLA Ops:
  0.6 0.7 copy-start.7
  2.7 0.7 copy-start.2
  2.7 0.7 copy-start.3
  3.5 0.8 copy-start
  4.3 0.7 copy-start.4
  4.3 0.7 copy-start.5
  4.3 0.7 copy-start.6
  140.5 0.8 copy-start.1
where the time goes:
time: 143 us; the launch traced here: 142 us
  Pallas kernels  134 us (94%)
  local copies, waits for them, and re-layouts  6.75 us (5%)
    pallas_call x1, Pallas kernels, on_device(): pl.pallas_call(functools.partial(kernel, counts, (tx, ty, tz), tile), out...  134 us

commit v1 on v0

v1 whole, which is shorter than its diff:
```python
import functools
import itertools
import math

import jax
import jax.numpy as jnp
from jax import lax
from jax.experimental import pallas as pl
from jax.experimental.pallas import tpu as pltpu
from jax.sharding import PartitionSpec as P

ITERS = 3
AXES = ("gx", "gy", "gz")
DIRECTIONS = [d for d in itertools.product((-1, 0, 1), repeat=3) if d != (0, 0, 0)]

LOG2E = math.log2(math.e)
coulomb_scale = 0.002 * math.sqrt(LOG2E)
response_scale = 0.003
SHIFT = 2.5


def sides(step, count, unit):
    if step < 0:
        return pl.ds(unit, unit), pl.ds((count + 1) * unit, unit)
    if step > 0:
        return pl.ds(count * unit, unit), pl.ds(0, unit)
    return pl.ds(unit, count * unit), pl.ds(unit, count * unit)


def kernel(
    counts, extent, tile,
    bits_ref, pos_ref, shield_ref, width_ref, hard_ref, soft_ref, coup_ref, rhs_ref,
    sol_ref, res_ref,
    store, par, basis, last, lhs, feats, shields, widths, acc, diag, sums, parts,
    halo_send, halo_recv, sum_send, sum_recv,
):
    tx, ty, tz = extent
    bf16, f32 = jnp.bfloat16, jnp.float32
    me = [lax.axis_index(axis) for axis in AXES]
    inside = pl.ds(tile, tz * tile)

    def lanes(c, n=1):
        if isinstance(c, int):
            return pl.ds(c * tile, n * tile)
        return pl.ds(pl.multiple_of(c * tile, tile), n * tile)

    def exists(d):
        ok = None
        for m, step, count in zip(me, d, counts):
            if step:
                here = (m + step >= 0) & (m + step < count)
                ok = here if ok is None else ok & here
        return ok

    def halo_copy(ref, slot, index, d):
        pairs = [sides(s, n, u) for s, n, u in zip(d, extent, (1, 1, tile))]
        source = (pairs[0][0], pairs[1][0], slice(None), pairs[2][0])
        target = (pairs[0][1], pairs[1][1], slice(None), pairs[2][1])
        return pltpu.make_async_remote_copy(
            src_ref=ref.at[source],
            dst_ref=ref.at[target],
            send_sem=halo_send.at[slot, index],
            recv_sem=halo_recv.at[slot, index],
            device_id=tuple(m + s for m, s in zip(me, d)),
            device_id_type=pl.DeviceIdType.MESH,
        )

    def halo_start(ref, slot):
        for index, d in enumerate(DIRECTIONS):
            @pl.when(exists(d))
            def _():
                halo_copy(ref, slot, index, d).start()

    def halo_fill(ref, fill):
        for d in DIRECTIONS:
            back = tuple(-s for s in d)
            strips = [sides(s, n, u)[1] for s, n, u in zip(back, extent, (1, 1, tile))]

            @pl.when(jnp.logical_not(exists(d)))
            def _():
                region = (strips[0], strips[1], slice(None), strips[2])
                ref[region] = jnp.full(ref.at[region].shape, fill, f32)

    def halo_wait(ref, slot):
        for index, d in enumerate(DIRECTIONS):
            @pl.when(exists(d))
            def _():
                halo_copy(ref, slot, index, d).wait_send()

            back = tuple(-s for s in d)

            @pl.when(exists(back))
            def _():
                halo_copy(ref, slot, index, d).wait_recv()

    rank = (me[0] * counts[1] + me[1]) * counts[2] + me[2]
    hops = [h for h in itertools.product(*map(range, counts)) if any(h)]

    def sum_copies(slot):
        return [
            pltpu.make_async_remote_copy(
                src_ref=sums.at[slot],
                dst_ref=parts.at[slot, rank],
                send_sem=sum_send.at[slot, j],
                recv_sem=sum_recv.at[slot, j],
                device_id=tuple(lax.rem(m + h, n) for m, h, n in zip(me, hop, counts)),
                device_id_type=pl.DeviceIdType.MESH,
            )
            for j, hop in enumerate(hops)
        ]

    column = lax.broadcasted_iota(jnp.int32, (4, tile), 1)

    def sum_start(slot, values):
        packed = jnp.zeros((4, tile), f32)
        for place, value in values.items():
            total = jnp.sum(value, axis=1, keepdims=True)
            packed = jnp.where(column == place, total, packed)
        sums[slot] = packed
        parts[slot, rank] = packed
        for copy in sum_copies(slot):
            copy.start()

    def sum_finish(slot, places):
        for copy in sum_copies(slot):
            copy.wait()
        value = jnp.sum(parts[slot], axis=0)
        value = value + jnp.concatenate([value[2:4], value[0:2]], axis=0)
        return {
            place: jnp.sum(jnp.where(column == place, value, 0.0), axis=1, keepdims=True)
            for place in places
        }

    row = lax.broadcasted_iota(jnp.int32, (8, tile), 0)
    blank = jnp.zeros((3, tile), f32)
    for a, b, c in itertools.product(range(tx), range(ty), range(tz)):
        par[a + 1, b + 1, :, lanes(c + 1)] = jnp.concatenate(
            [
                pos_ref[:, a, b, c, :] - 0.5,
                shield_ref[a, b, c : c + 1, :] * math.sqrt(LOG2E),
                width_ref[a, b, c : c + 1, :],
                blank,
            ],
            axis=0,
        )
        basis[0, a + 1, b + 1, :, lanes(c + 1)] = rhs_ref[:, a, b, c, :]
    halo_start(par, 0)
    halo_start(basis.at[0], 1)
    halo_fill(par, 0.5)
    for k in range(ITERS):
        halo_fill(basis.at[k], 0.0)

    def rounded(value):
        return value.astype(bf16).astype(f32)

    def prepare(ap, bp, cp):
        raw = par[ap, bp, :, lanes(cp)]
        scaled = raw * (2 * LOG2E)
        high = rounded(scaled)
        low = scaled - high
        squares = raw * raw
        norm = (squares[0:1] + squares[1:2] + squares[2:3]) * -LOG2E
        norm_high = rounded(norm)
        first = jnp.where(
            row < 3, high, jnp.where(row == 3, norm_high, jnp.where(row == 4, norm - norm_high, 1.0))
        )
        second = jnp.where(row < 3, high, 0.0)
        third = jnp.where(row < 3, low, 0.0)
        turned = jnp.concatenate([first, second, third, third, raw], axis=0).T
        feats[cp] = turned[:, :32].astype(bf16)
        shields[cp] = jnp.broadcast_to(turned[:, 35:36], (tile, tile))
        widths[cp] = jnp.broadcast_to(turned[:, 36:37], (tile, tile))

    same = lax.broadcasted_iota(jnp.int32, (tile, tile), 0) == lax.broadcasted_iota(
        jnp.int32, (tile, tile), 1
    )

    def pair_rows(ap, bp, a, b, sources):
        oa, ob = ap - 1 - a, bp - 1 - b
        fa, fb = oa.astype(f32), ob.astype(f32)
        offset = jnp.where(row == 0, fa, jnp.where(row == 1, fb, 0.0))
        group = (oa + 1) * 3 + (ob + 1)
        centre = group == 4
        base = (a * ty + b) * tz

        def target(c):
            own = par[a + 1, b + 1, :, lanes(c + 1)]
            grid = jnp.round(own * 128.0) * (1.0 / 128.0)
            rest = own - grid
            moved = own - offset
            squares = moved * moved
            plane = squares[0:1] + squares[1:2]
            bits = bits_ref[a, b, c]
            return own, grid - offset, jnp.where(row < 3, rest, 0.0), plane, own[2:3], bits

        def factors(parts_of, step):
            own, grid, rest, plane, height, bits = parts_of
            shifted = jnp.where(row == 2, grid - float(step), grid)
            norm = (plane + (height - float(step)) * (height - float(step))) * -LOG2E
            norm_high = rounded(norm)
            listed = (jnp.right_shift(bits, group * 3 + (step + 1)) & 1) == 1
            mask = jnp.where(listed, 0.0, -jnp.inf)
            first = jnp.where(row < 3, shifted, jnp.where(row < 5, 1.0, mask))
            first = jnp.where(row == 5, norm_high, jnp.where(row == 6, norm - norm_high, first))
            third = jnp.where(row < 3, shifted, 0.0)
            return jnp.concatenate([first, rest, third, rest], axis=0).astype(bf16)

        held = {}
        for cp in sources:
            cells = [c for c in (cp - 2, cp - 1, cp) if 0 <= c < tz]
            for c in cells:
                if c not in held:
                    held[c] = target(c)
            right = jnp.concatenate([factors(held[c], cp - 1 - c) for c in cells], axis=1)
            got = jnp.dot(feats[cp], right, preferred_element_type=f32)
            for n, c in enumerate(cells):
                own = held[c][0]
                energy = got[:, n * tile : (n + 1) * tile]
                reach = (shields[cp] * own[3:4] - energy).astype(bf16)
                span = (widths[cp] + own[4:5]).astype(bf16)
                coulomb = lax.rsqrt(reach)
                response = jnp.exp2(energy.astype(bf16) / span)
                if cp - 1 == c:
                    drop = same & centre
                    coulomb = jnp.where(drop, jnp.zeros_like(coulomb), coulomb)
                    response = jnp.where(drop, jnp.zeros_like(response), response)
                start = group * (3 * tile) + (cp - c) * tile
                rows = pl.ds(pl.multiple_of(start, tile), tile)
                store[base + c, rows, 0:tile] = coulomb
                store[base + c, rows, tile : 2 * tile] = response

    def source_row(ap, bp, sources):
        for cp in sources:
            prepare(ap, bp, cp)
        a_low, b_low = jnp.maximum(ap - 2, 0), jnp.maximum(bp - 2, 0)
        wide = jnp.minimum(bp, ty - 1) + 1 - b_low
        total = (jnp.minimum(ap, tx - 1) + 1 - a_low) * wide

        def step(n, carry):
            pair_rows(ap, bp, a_low + n // wide, b_low + n % wide, sources)
            return carry

        lax.fori_loop(0, total, step, 0)

    def own_rows(sources):
        def over(q, carry):
            source_row(1 + q // ty, 1 + q % ty, sources)
            return carry

        lax.fori_loop(0, tx * ty, over, 0)

    own_rows(list(range(1, tz + 1)))
    halo_wait(par, 0)
    own_rows([0, tz + 1])

    def ghost_row(q, carry):
        ap = q // (ty + 2)
        bp = q % (ty + 2)
        own = (ap >= 1) & (ap <= tx) & (bp >= 1) & (bp <= ty)
        held = (ap + me[0] >= 1) & (ap + me[0] <= tx + counts[0] - 1)
        held = held & (bp + me[1] >= 1) & (bp + me[1] <= ty + counts[1] - 1)

        @pl.when(jnp.logical_not(own) & held)
        def _():
            source_row(ap, bp, list(range(tz + 2)))

        return carry

    lax.fori_loop(0, (tx + 2) * (ty + 2), ghost_row, 0)

    def split(value):
        upper = rounded(value)
        ones = jnp.ones((8, value.shape[1]), f32)
        return jnp.concatenate([upper, value - upper, ones], axis=0).astype(bf16)

    def split_all(k):
        def one(q, carry):
            ap = q // (ty + 2)
            bp = q % (ty + 2)
            lhs[ap, bp] = split(basis[k, ap, bp])
            return carry

        lax.fori_loop(0, (tx + 2) * (ty + 2), one, 0)

    charge_rows = lax.broadcasted_iota(jnp.int32, (4, tile), 0) < 2
    low_side = [m > 0 for m in me]
    high_side = [m < n - 1 for m, n in zip(me, counts)]

    def near(place, count):
        return [p for p in (place, place + 1, place + 2)], count

    def operate(k):
        norm = product = jnp.zeros((4, tile), f32)
        for a, b in itertools.product(range(tx), range(ty)):
            groups = {}
            for ap, bp in itertools.product(range(a, a + 3), range(b, b + 3)):
                key = (
                    -1 if ap == 0 else int(ap == tx + 1),
                    -1 if bp == 0 else int(bp == ty + 1),
                )
                groups.setdefault(key, []).append((ap, bp))
            base = (a * ty + b) * tz

            def gather(pairs, c, first):
                left = jnp.concatenate([lhs[ap, bp, :, lanes(c, 3)] for ap, bp in pairs], axis=1)
                right = jnp.concatenate(
                    [
                        store[base + c, pl.ds(((ap - a) * 3 + bp - b) * 3 * tile, 3 * tile), :]
                        for ap, bp in pairs
                    ],
                    axis=0,
                )
                got = jnp.dot(left, right, preferred_element_type=f32)
                acc[c] = got if first else acc[c] + got

            for c in range(tz):
                gather(groups[0, 0], c, True)
            for key, pairs in groups.items():
                if key == (0, 0):
                    continue
                there = None
                for m, step in enumerate(key):
                    if step:
                        side = (low_side if step < 0 else high_side)[m]
                        there = side if there is None else there & side

                @pl.when(there)
                def _():
                    for c in range(tz):
                        gather(pairs, c, False)

            for c in range(tz):
                got = acc[c]
                pair = got[0:4] + got[4:8]
                pair = jnp.where(
                    charge_rows, pair[:, :tile] * coulomb_scale, pair[:, tile:] * -response_scale
                )
                here = lanes(c)
                if k == 0:
                    row_sums = jnp.where(
                        charge_rows,
                        got[8:12, :tile] * coulomb_scale + hard_ref[a, b, c : c + 1, :],
                        got[8:12, tile:] * response_scale + soft_ref[a, b, c : c + 1, :],
                    )
                    diag[a, b, :, here] = row_sums - SHIFT
                vector = basis[k, a + 1, b + 1, :, lanes(c + 1)]
                swapped = jnp.concatenate([vector[2:4], vector[0:2]], axis=0)
                link = coup_ref[a, b, c : c + 1, :]
                image = diag[a, b, :, here] * vector + pair + link * swapped
                if k + 1 < ITERS:
                    basis[k + 1, a + 1, b + 1, :, lanes(c + 1)] = image
                else:
                    last[a, b, :, here] = image
                norm = norm + image * image
                product = product + vector * image
        return norm, product

    start_norm = jnp.zeros((4, tile), f32)
    for a, b, c in itertools.product(range(tx), range(ty), range(tz)):
        value = basis[0, a + 1, b + 1, :, lanes(c + 1)]
        start_norm = start_norm + value * value
    moments = {0: start_norm}
    for k in range(ITERS):
        halo_wait(basis.at[k], 1 + k)
        split_all(k)
        norm, product = operate(k)
        moments[2 * k + 1] = product
        if k + 1 < ITERS:
            moments[2 * k + 2] = norm
            halo_start(basis.at[k + 1], 2 + k)
        if k + 2 == ITERS:
            sum_start(0, moments)
            early, moments = list(moments), {}
    sum_start(1, moments)
    gram = sum_finish(0, early)
    gram.update(sum_finish(1, list(moments)))
    gram = {n: jnp.broadcast_to(value, (4, tile)) for n, value in gram.items()}

    def dot(left, right):
        total = None
        for (i, x), (j, y) in itertools.product(enumerate(left), enumerate(right)):
            term = x * y * gram[i + j]
            total = term if total is None else total + term
        return total

    def combined(left, scale, right):
        size = max(len(left), len(right))
        out = []
        for i in range(size):
            if i >= len(left):
                out.append(scale * right[i])
            elif i >= len(right):
                out.append(left[i])
            else:
                out.append(left[i] + scale * right[i])
        return out

    one = jnp.ones((4, tile), f32)
    rem, along, found = [one], [one], []
    norm_now = gram[0]
    for k in range(ITERS):
        image = combined([SHIFT * x for x in along], one, [jnp.zeros_like(one)] + along)
        step_size = norm_now / dot(along, image)
        found = combined(found, step_size, along)
        rem = combined(rem, -step_size, image)
        if k + 1 < ITERS:
            norm_next = dot(rem, rem)
            along = combined(rem, norm_next / norm_now, along)
            norm_now = norm_next

    for a, b, c in itertools.product(range(tx), range(ty), range(tz)):
        held = [basis[k, a + 1, b + 1, :, lanes(c + 1)] for k in range(ITERS)]
        held.append(last[a, b, :, lanes(c)])
        sol_ref[:, a, b, c, :] = sum(x * v for x, v in zip(found, held))
        res_ref[:, a, b, c, :] = sum(x * v for x, v in zip(rem, held))


def on_device(counts, positions, shield, width, hardness, softness, coupling, pair_bits, right_side):
    tx, ty, tz, tile = hardness.shape
    padded = (tx + 2, ty + 2)
    width_lanes = (tz + 2) * tile
    peers = counts[0] * counts[1] * counts[2]
    field = jax.ShapeDtypeStruct((4, tx, ty, tz, tile), jnp.float32)
    vmem = pl.BlockSpec(memory_space=pltpu.VMEM)
    return pl.pallas_call(
        functools.partial(kernel, counts, (tx, ty, tz), tile),
        out_shape=(field, field),
        in_specs=[pl.BlockSpec(memory_space=pltpu.SMEM)] + [vmem] * 7,
        out_specs=(vmem, vmem),
        scratch_shapes=[
            pltpu.VMEM((tx * ty * tz, 27 * tile, 2 * tile), jnp.bfloat16),
            pltpu.VMEM(padded + (8, width_lanes), jnp.float32),
            pltpu.VMEM((ITERS,) + padded + (4, width_lanes), jnp.float32),
            pltpu.VMEM((tx, ty, 4, tz * tile), jnp.float32),
            pltpu.VMEM(padded + (16, width_lanes), jnp.bfloat16),
            pltpu.VMEM((tz + 2, tile, 32), jnp.bfloat16),
            pltpu.VMEM((tz + 2, tile, tile), jnp.float32),
            pltpu.VMEM((tz + 2, tile, tile), jnp.float32),
            pltpu.VMEM((tz, 16, 2 * tile), jnp.float32),
            pltpu.VMEM((tx, ty, 4, tz * tile), jnp.float32),
            pltpu.VMEM((2, 4, tile), jnp.float32),
            pltpu.VMEM((2, peers, 4, tile), jnp.float32),
            pltpu.SemaphoreType.DMA((ITERS + 1, 26)),
            pltpu.SemaphoreType.DMA((ITERS + 1, 26)),
            pltpu.SemaphoreType.DMA((2, peers)),
            pltpu.SemaphoreType.DMA((2, peers)),
        ],
        compiler_params=pltpu.CompilerParams(
            has_side_effects=True, vmem_limit_bytes=67043328
        ),
    )(pair_bits, positions, shield, width, hardness, softness, coupling, right_side)


def solution(mesh):
    counts = tuple(mesh.shape[axis] for axis in AXES)
    tiles = P("gx", "gy", "gz", None)
    four = P(None, "gx", "gy", "gz", None)
    return jax.shard_map(
        functools.partial(on_device, counts),
        mesh=mesh,
        in_specs=(four, tiles, tiles, tiles, tiles, tiles, P("gx", "gy", "gz"), four),
        out_specs=(four, four),
        check_vma=False,
    )
```

time: 143 us -> 91.7 us (0.64)
  Pallas kernels: 134 us -> 88.7 us
  local copies, waits for them, and re-layouts: 6.75 us -> 2.14 us
    pallas_call x1, Pallas kernels: 134 us -> 88.7 us  [on_device(): pl.pallas_call(functools.partial(kernel, counts, (tx, ty, tz), tile), out...]
    reshape x5 -> x0, local copies, waits for them, and re-layouts: 2.82 us -> none  [the longest x4 2.16 us: fields(): return x.reshape(tx, ty, 4, tz, tile).transpose(2, 0, 1, 3, 4)]
where the time goes in v1:
time: 91.7 us; the launch traced here: 91.5 us
  Pallas kernels  88.7 us (97%)
  local copies, waits for them, and re-layouts  2.14 us (2%)
    pallas_call x1, Pallas kernels, on_device(): pl.pallas_call(functools.partial(kernel, counts, (tx, ty, tz), tile), out...  88.7 us
    unnamed x4, local copies, waits for them, and re-layouts  2.14 us

profile of v1, /device:TPU:0, one launch (start us, length us, event | category | flops | bytes accessed | tf_op | source)
XLA Modules:
  0.0 91.5 jit_solution(15445327327428734846)
XLA Ops:
  0.6 88.7 %shard_map.95 = (f32[4,2,2,8,128]{4,3,2,1,0:T(8,128)}, f32[4,2,2,8,128]{4,3,2,1,0:T(8,128)}) custom-call(s32[2,2,8]{2,1,0:T(2,128)} %bits_ref.1, f32[3,2,2,8,128]{4,3,2,1,0:T(8,128)} %pos_ref.1, f32[2,2,8,128]{3,2,1,0:T(8,128)} %shield_ref.1, f32[2,2,8,128]{3,2,1,0:T(8,128)} %width_ref.1, f32[2,2,8,128]{3,2,1,0:T(8,128)} %hard_ref.1, ...), custom_call_target="tpu_custom_call" | custom-call | tf_op jit(solution)/shard_map/pallas_call | solution.py:425
  89.3 0.0 copy-start
  89.3 1.5 %copy.12 = f32[4,2,2,8,128]{4,3,2,1,0:T(8,128)} copy(f32[4,2,2,8,128]{4,3,2,1,0:T(8,128)} %get-tuple-element.4) | data formatting | bytes 131072
  90.8 0.0 copy-done
  90.8 0.6 copy.13
Async XLA Ops:
  89.3 1.5 %copy-start = (f32[4,2,2,8,128]{4,3,2,1,0:T(8,128)S(1)}, f32[4,2,2,8,128]{4,3,2,1,0:T(8,128)}, u32[]{:S(2)}) copy-start(f32[4,2,2,8,128]{4,3,2,1,0:T(8,128)} %get-tuple-element.5) | copy-start | bytes 196612

commit v2 on v1

--- a/solution.py
+++ b/solution.py
@@ -131,6 +131,15 @@
             for place in places
         }
 
+    barrier = pltpu.get_barrier_semaphore()
+    for hop in hops:
+        pl.semaphore_signal(
+            barrier,
+            inc=1,
+            device_id=tuple(lax.rem(m + h, n) for m, h, n in zip(me, hop, counts)),
+            device_id_type=pl.DeviceIdType.MESH,
+        )
+
     row = lax.broadcasted_iota(jnp.int32, (8, tile), 0)
     blank = jnp.zeros((3, tile), f32)
     for a, b, c in itertools.product(range(tx), range(ty), range(tz)):
@@ -144,8 +153,6 @@
             axis=0,
         )
         basis[0, a + 1, b + 1, :, lanes(c + 1)] = rhs_ref[:, a, b, c, :]
-    halo_start(par, 0)
-    halo_start(basis.at[0], 1)
     halo_fill(par, 0.5)
     for k in range(ITERS):
         halo_fill(basis.at[k], 0.0)
@@ -226,8 +233,8 @@
                     response = jnp.where(drop, jnp.zeros_like(response), response)
                 start = group * (3 * tile) + (cp - c) * tile
                 rows = pl.ds(pl.multiple_of(start, tile), tile)
-                store[base + c, rows, 0:tile] = coulomb
-                store[base + c, rows, tile : 2 * tile] = response
+                store[base + c, 0, rows, :] = coulomb
+                store[base + c, 1, rows, :] = response
 
     def source_row(ap, bp, sources):
         for cp in sources:
@@ -242,16 +249,20 @@
 
         lax.fori_loop(0, total, step, 0)
 
-    def own_rows(sources):
+    def own_rows(first, stop, sources):
         def over(q, carry):
             source_row(1 + q // ty, 1 + q % ty, sources)
             return carry
 
-        lax.fori_loop(0, tx * ty, over, 0)
-
-    own_rows(list(range(1, tz + 1)))
+        lax.fori_loop(first, stop, over, 0)
+
+    own_rows(0, 1, list(range(1, tz + 1)))
+    pl.semaphore_wait(barrier, len(hops))
+    halo_start(par, 0)
+    halo_start(basis.at[0], 1)
+    own_rows(1, tx * ty, list(range(1, tz + 1)))
     halo_wait(par, 0)
-    own_rows([0, tz + 1])
+    own_rows(0, tx * ty, [0, tz + 1])
 
     def ghost_row(q, carry):
         ap = q // (ty + 2)
@@ -273,48 +284,66 @@
         ones = jnp.ones((8, value.shape[1]), f32)
         return jnp.concatenate([upper, value - upper, ones], axis=0).astype(bf16)
 
-    def split_all(k):
-        def one(q, carry):
-            ap = q // (ty + 2)
-            bp = q % (ty + 2)
-            lhs[ap, bp] = split(basis[k, ap, bp])
-            return carry
-
-        lax.fori_loop(0, (tx + 2) * (ty + 2), one, 0)
+    def split_rows(k, places, cells):
+        for ap, bp in places:
+            for cp in cells:
+                lhs[k % 2, ap, bp, cp] = split(basis[k, ap, bp, :, lanes(cp)])
+
+    every = list(itertools.product(range(tx + 2), range(ty + 2)))
+    own_places = [(ap, bp) for ap, bp in every if 1 <= ap <= tx and 1 <= bp <= ty]
+    ghost_places = [p for p in every if p not in own_places]
+
+    def split_ghosts(k):
+        split_rows(k, own_places, (0, tz + 1))
+        split_rows(k, ghost_places, range(tz + 2))
 
     charge_rows = lax.broadcasted_iota(jnp.int32, (4, tile), 0) < 2
     low_side = [m > 0 for m in me]
     high_side = [m < n - 1 for m, n in zip(me, counts)]
 
-    def near(place, count):
-        return [p for p in (place, place + 1, place + 2)], count
-
-    def operate(k):
+    def neighbours(a, b):
+        groups = {}
+        for ap, bp in itertools.product(range(a, a + 3), range(b, b + 3)):
+            key = (
+                -1 if ap == 0 else int(ap == tx + 1),
+                -1 if bp == 0 else int(bp == ty + 1),
+            )
+            groups.setdefault(key, []).append((ap, bp))
+        return groups
+
+    tiles_of = [(a, b, (a * ty + b) * tz) for a, b in itertools.product(range(tx), range(ty))]
+
+    def gather(k, a, b, base, pairs, c, first):
+        left = jnp.concatenate(
+            [lhs[k % 2, ap, bp, c + n] for ap, bp in pairs for n in range(3)], axis=1
+        )
+        right = jnp.concatenate(
+            [
+                jnp.concatenate(
+                    [
+                        store[base + c, f, pl.ds(((ap - a) * 3 + bp - b) * 3 * tile, 3 * tile), :]
+                        for f in range(2)
+                    ],
+                    axis=1,
+                )
+                for ap, bp in pairs
+            ],
+            axis=0,
+        )
+        got = jnp.dot(left, right, preferred_element_type=f32)
+        acc[base + c] = got if first else acc[base + c] + got
+
+    def operate_inside(k):
+        for a, b, base in tiles_of:
+            for c in range(1, tz - 1):
+                gather(k, a, b, base, neighbours(a, b)[0, 0], c, True)
+
+    def operate_outside(k):
         norm = product = jnp.zeros((4, tile), f32)
-        for a, b in itertools.product(range(tx), range(ty)):
-            groups = {}
-            for ap, bp in itertools.product(range(a, a + 3), range(b, b + 3)):
-                key = (
-                    -1 if ap == 0 else int(ap == tx + 1),
-                    -1 if bp == 0 else int(bp == ty + 1),
-                )
-                groups.setdefault(key, []).append((ap, bp))
-            base = (a * ty + b) * tz
-
-            def gather(pairs, c, first):
-                left = jnp.concatenate([lhs[ap, bp, :, lanes(c, 3)] for ap, bp in pairs], axis=1)
-                right = jnp.concatenate(
-                    [
-                        store[base + c, pl.ds(((ap - a) * 3 + bp - b) * 3 * tile, 3 * tile), :]
-                        for ap, bp in pairs
-                    ],
-                    axis=0,
-                )
-                got = jnp.dot(left, right, preferred_element_type=f32)
-                acc[c] = got if first else acc[c] + got
-
-            for c in range(tz):
-                gather(groups[0, 0], c, True)
+        for a, b, base in tiles_of:
+            groups = neighbours(a, b)
+            for c in sorted({0, tz - 1}):
+                gather(k, a, b, base, groups[0, 0], c, True)
             for key, pairs in groups.items():
                 if key == (0, 0):
                     continue
@@ -327,10 +356,10 @@
                 @pl.when(there)
                 def _():
                     for c in range(tz):
-                        gather(pairs, c, False)
+                        gather(k, a, b, base, pairs, c, False)
 
             for c in range(tz):
-                got = acc[c]
+                got = acc[base + c]
                 pair = got[0:4] + got[4:8]
                 pair = jnp.where(
                     charge_rows, pair[:, :tile] * coulomb_scale, pair[:, tile:] * -response_scale
@@ -349,6 +378,7 @@
                 image = diag[a, b, :, here] * vector + pair + link * swapped
                 if k + 1 < ITERS:
                     basis[k + 1, a + 1, b + 1, :, lanes(c + 1)] = image
+                    lhs[(k + 1) % 2, a + 1, b + 1, c + 1] = split(image)
                 else:
                     last[a, b, :, here] = image
                 norm = norm + image * image
@@ -360,10 +390,12 @@
         value = basis[0, a + 1, b + 1, :, lanes(c + 1)]
         start_norm = start_norm + value * value
     moments = {0: start_norm}
+    split_rows(0, own_places, range(1, tz + 1))
     for k in range(ITERS):
+        operate_inside(k)
         halo_wait(basis.at[k], 1 + k)
-        split_all(k)
-        norm, product = operate(k)
+        split_ghosts(k)
+        norm, product = operate_outside(k)
         moments[2 * k + 1] = product
         if k + 1 < ITERS:
             moments[2 * k + 2] = norm
@@ -428,15 +460,15 @@
         in_specs=[pl.BlockSpec(memory_space=pltpu.SMEM)] + [vmem] * 7,
         out_specs=(vmem, vmem),
         scratch_shapes=[
-            pltpu.VMEM((tx * ty * tz, 27 * tile, 2 * tile), jnp.bfloat16),
+            pltpu.VMEM((tx * ty * tz, 2, 27 * tile, tile), jnp.bfloat16),
             pltpu.VMEM(padded + (8, width_lanes), jnp.float32),
             pltpu.VMEM((ITERS,) + padded + (4, width_lanes), jnp.float32),
             pltpu.VMEM((tx, ty, 4, tz * tile), jnp.float32),
-            pltpu.VMEM(padded + (16, width_lanes), jnp.bfloat16),
+            pltpu.VMEM((2,) + padded + (tz + 2, 16, tile), jnp.bfloat16),
             pltpu.VMEM((tz + 2, tile, 32), jnp.bfloat16),
             pltpu.VMEM((tz + 2, tile, tile), jnp.float32),
             pltpu.VMEM((tz + 2, tile, tile), jnp.float32),
-            pltpu.VMEM((tz, 16, 2 * tile), jnp.float32),
+            pltpu.VMEM((tx * ty * tz, 16, 2 * tile), jnp.float32),
             pltpu.VMEM((tx, ty, 4, tz * tile), jnp.float32),
             pltpu.VMEM((2, 4, tile), jnp.float32),
             pltpu.VMEM((2, peers, 4, tile), jnp.float32),
@@ -446,7 +478,7 @@
             pltpu.SemaphoreType.DMA((2, peers)),
         ],
         compiler_params=pltpu.CompilerParams(
-            has_side_effects=True, vmem_limit_bytes=67043328
+            collective_id=0, has_side_effects=True, vmem_limit_bytes=67043328
         ),
     )(pair_bits, positions, shield, width, hardness, softness, coupling, right_side)
 

time: 91.7 us -> 80.4 us (0.88)
  Pallas kernels: 88.7 us -> 77.4 us
    pallas_call x1, Pallas kernels: 88.7 us -> 77.4 us  [on_device(): pl.pallas_call(functools.partial(kernel, counts, (tx, ty, tz), tile), out...]
where the time goes in v2:
time: 80.4 us; the launch traced here: 80.2 us
  Pallas kernels  77.4 us (96%)
  local copies, waits for them, and re-layouts  2.14 us (3%)
    pallas_call x1, Pallas kernels, on_device(): pl.pallas_call(functools.partial(kernel, counts, (tx, ty, tz), tile), out...  77.4 us
    unnamed x4, local copies, waits for them, and re-layouts  2.14 us

profile of v2, /device:TPU:0, one launch (start us, length us, event | category | flops | bytes accessed | tf_op | source)
XLA Modules:
  0.0 80.2 jit_solution(6439625283747231213)
XLA Ops:
  0.6 77.4 %shard_map.95 = (f32[4,2,2,8,128]{4,3,2,1,0:T(8,128)}, f32[4,2,2,8,128]{4,3,2,1,0:T(8,128)}) custom-call(s32[2,2,8]{2,1,0:T(2,128)} %bits_ref.1, f32[3,2,2,8,128]{4,3,2,1,0:T(8,128)} %pos_ref.1, f32[2,2,8,128]{3,2,1,0:T(8,128)} %shield_ref.1, f32[2,2,8,128]{3,2,1,0:T(8,128)} %width_ref.1, f32[2,2,8,128]{3,2,1,0:T(8,128)} %hard_ref.1, ...), custom_call_target="tpu_custom_call" | custom-call | tf_op jit(solution)/shard_map/pallas_call | solution.py:457
  78.0 0.0 copy-start
  78.0 1.5 %copy.12 = f32[4,2,2,8,128]{4,3,2,1,0:T(8,128)} copy(f32[4,2,2,8,128]{4,3,2,1,0:T(8,128)} %get-tuple-element.4) | data formatting | bytes 131072
  79.5 0.0 copy-done
  79.5 0.6 copy.13
Async XLA Ops:
  78.0 1.5 %copy-start = (f32[4,2,2,8,128]{4,3,2,1,0:T(8,128)S(1)}, f32[4,2,2,8,128]{4,3,2,1,0:T(8,128)}, u32[]{:S(2)}) copy-start(f32[4,2,2,8,128]{4,3,2,1,0:T(8,128)} %get-tuple-element.5) | copy-start | bytes 196612

commit v3 on v2

--- a/solution.py
+++ b/solution.py
@@ -30,8 +30,8 @@
 def kernel(
     counts, extent, tile,
     bits_ref, pos_ref, shield_ref, width_ref, hard_ref, soft_ref, coup_ref, rhs_ref,
-    sol_ref, res_ref,
-    store, par, basis, last, lhs, feats, shields, widths, acc, diag, sums, parts,
+    out_ref,
+    store, par, basis, last, lhs, feats, columns, picker, energies, acc, diag, sums, parts,
     halo_send, halo_recv, sum_send, sum_recv,
 ):
     tx, ty, tz = extent
@@ -110,12 +110,14 @@
         ]
 
     column = lax.broadcasted_iota(jnp.int32, (4, tile), 1)
+    field = lax.broadcasted_iota(jnp.int32, (4, tile), 0)
 
     def sum_start(slot, values):
         packed = jnp.zeros((4, tile), f32)
         for place, value in values.items():
             total = jnp.sum(value, axis=1, keepdims=True)
-            packed = jnp.where(column == place, total, packed)
+            packed = jnp.where(column == 4 * place + field, total, packed)
+        packed = jnp.sum(packed, axis=0, keepdims=True)
         sums[slot] = packed
         parts[slot, rank] = packed
         for copy in sum_copies(slot):
@@ -124,10 +126,10 @@
     def sum_finish(slot, places):
         for copy in sum_copies(slot):
             copy.wait()
-        value = jnp.sum(parts[slot], axis=0)
-        value = value + jnp.concatenate([value[2:4], value[0:2]], axis=0)
+        value = jnp.broadcast_to(jnp.sum(parts[slot], axis=0), (4, tile))
+        value = jnp.where(column % 2 == field % 2, value, 0.0)
         return {
-            place: jnp.sum(jnp.where(column == place, value, 0.0), axis=1, keepdims=True)
+            place: jnp.sum(jnp.where(column // 4 == place, value, 0.0), axis=1, keepdims=True)
             for place in places
         }
 
@@ -160,6 +162,10 @@
     def rounded(value):
         return value.astype(bf16).astype(f32)
 
+    slab = lax.broadcasted_iota(jnp.int32, (32, 2 * tile), 0)
+    half = lax.broadcasted_iota(jnp.int32, (32, 2 * tile), 1) // tile
+    picker[...] = jnp.where((slab >= 8) & (slab % 8 == 3 + half), 1.0, 0.0).astype(bf16)
+
     def prepare(ap, bp, cp):
         raw = par[ap, bp, :, lanes(cp)]
         scaled = raw * (2 * LOG2E)
@@ -171,24 +177,32 @@
         first = jnp.where(
             row < 3, high, jnp.where(row == 3, norm_high, jnp.where(row == 4, norm - norm_high, 1.0))
         )
-        second = jnp.where(row < 3, high, 0.0)
-        third = jnp.where(row < 3, low, 0.0)
-        turned = jnp.concatenate([first, second, third, third, raw], axis=0).T
-        feats[cp] = turned[:, :32].astype(bf16)
-        shields[cp] = jnp.broadcast_to(turned[:, 35:36], (tile, tile))
-        widths[cp] = jnp.broadcast_to(turned[:, 36:37], (tile, tile))
+        part = rounded(raw)
+        rest = raw - part
+        middle = rounded(rest)
+        second = jnp.where(row < 3, high, jnp.where(row < 5, part, 0.0))
+        third = jnp.where(row < 3, low, jnp.where(row < 5, middle, 0.0))
+        fourth = jnp.where(row < 3, low, jnp.where(row < 5, rest - middle, 0.0))
+        turned = jnp.concatenate([first, second, third, fourth], axis=0).T.astype(bf16)
+        feats[cp] = turned
+        columns[cp] = jnp.dot(turned, picker[...], preferred_element_type=f32)
 
     same = lax.broadcasted_iota(jnp.int32, (tile, tile), 0) == lax.broadcasted_iota(
         jnp.int32, (tile, tile), 1
     )
 
-    def pair_rows(ap, bp, a, b, sources):
+    def place_of(ap, bp, a, b):
         oa, ob = ap - 1 - a, bp - 1 - b
+        group = (oa + 1) * 3 + (ob + 1)
+        return oa, ob, group, (a * ty + b) * tz
+
+    def cells_of(cp):
+        return [c for c in (cp - 2, cp - 1, cp) if 0 <= c < tz]
+
+    def measure_rows(ap, bp, a, b, sources, slot):
+        oa, ob, group, _ = place_of(ap, bp, a, b)
         fa, fb = oa.astype(f32), ob.astype(f32)
         offset = jnp.where(row == 0, fa, jnp.where(row == 1, fb, 0.0))
-        group = (oa + 1) * 3 + (ob + 1)
-        centre = group == 4
-        base = (a * ty + b) * tz
 
         def target(c):
             own = par[a + 1, b + 1, :, lanes(c + 1)]
@@ -214,55 +228,80 @@
 
         held = {}
         for cp in sources:
-            cells = [c for c in (cp - 2, cp - 1, cp) if 0 <= c < tz]
+            cells = cells_of(cp)
             for c in cells:
                 if c not in held:
                     held[c] = target(c)
             right = jnp.concatenate([factors(held[c], cp - 1 - c) for c in cells], axis=1)
             got = jnp.dot(feats[cp], right, preferred_element_type=f32)
-            for n, c in enumerate(cells):
-                own = held[c][0]
-                energy = got[:, n * tile : (n + 1) * tile]
-                reach = (shields[cp] * own[3:4] - energy).astype(bf16)
-                span = (widths[cp] + own[4:5]).astype(bf16)
+            for m in range(len(cells)):
+                energies[slot + m] = got[:, m * tile : (m + 1) * tile]
+            slot += len(cells)
+
+    def fill_rows(ap, bp, a, b, sources, slot):
+        _, _, group, base = place_of(ap, bp, a, b)
+        centre = group == 4
+        for cp in sources:
+            for c in cells_of(cp):
+                own = par[a + 1, b + 1, :, lanes(c + 1)]
+                energy = energies[slot].astype(bf16)
+                slot += 1
+                reach = (columns[cp, :, :tile] * own[3:4]).astype(bf16) - energy
+                span = (columns[cp, :, tile:] + own[4:5]).astype(bf16)
                 coulomb = lax.rsqrt(reach)
-                response = jnp.exp2(energy.astype(bf16) / span)
+                response = jnp.exp2(energy / span)
                 if cp - 1 == c:
                     drop = same & centre
                     coulomb = jnp.where(drop, jnp.zeros_like(coulomb), coulomb)
                     response = jnp.where(drop, jnp.zeros_like(response), response)
                 start = group * (3 * tile) + (cp - c) * tile
                 rows = pl.ds(pl.multiple_of(start, tile), tile)
-                store[base + c, 0, rows, :] = coulomb
-                store[base + c, 1, rows, :] = response
-
-    def source_row(ap, bp, sources):
+                store[base + c, rows, :] = jnp.concatenate([coulomb, response], axis=1)
+
+    def several(ap, bp, places, sources):
+        each = sum(len(cells_of(cp)) for cp in sources)
+        for n, (a, b) in enumerate(places):
+            measure_rows(ap, bp, a, b, sources, n * each)
+        for n, (a, b) in enumerate(places):
+            fill_rows(ap, bp, a, b, sources, n * each)
+
+    def source_row(ap, bp, sources, least=1):
         for cp in sources:
             prepare(ap, bp, cp)
         a_low, b_low = jnp.maximum(ap - 2, 0), jnp.maximum(bp - 2, 0)
         wide = jnp.minimum(bp, ty - 1) + 1 - b_low
         total = (jnp.minimum(ap, tx - 1) + 1 - a_low) * wide
 
+        def place(n):
+            return a_low + n // wide, b_low + n % wide
+
         def step(n, carry):
-            pair_rows(ap, bp, a_low + n // wide, b_low + n % wide, sources)
+            several(ap, bp, [place(least * n + m) for m in range(least)], sources)
             return carry
 
-        lax.fori_loop(0, total, step, 0)
-
-    def own_rows(first, stop, sources):
+        def single(n, carry):
+            several(ap, bp, [place(total - 1)], sources)
+            return carry
+
+        lax.fori_loop(0, total // least, step, 0)
+        if least == 2 and not (tx <= 2 and ty <= 2 and len(sources) == tz):
+            lax.fori_loop(0, total % 2, single, 0)
+
+    def own_rows(first, stop, sources, least):
         def over(q, carry):
-            source_row(1 + q // ty, 1 + q % ty, sources)
+            source_row(1 + q // ty, 1 + q % ty, sources, least)
             return carry
 
         lax.fori_loop(first, stop, over, 0)
 
-    own_rows(0, 1, list(range(1, tz + 1)))
+    pairs = 2 if tx == 2 and ty == 2 else 1
+    own_rows(0, 1, list(range(1, tz + 1)), pairs)
     pl.semaphore_wait(barrier, len(hops))
     halo_start(par, 0)
     halo_start(basis.at[0], 1)
-    own_rows(1, tx * ty, list(range(1, tz + 1)))
+    own_rows(1, tx * ty, list(range(1, tz + 1)), pairs)
     halo_wait(par, 0)
-    own_rows(0, tx * ty, [0, tz + 1])
+    own_rows(0, tx * ty, [0, tz + 1], 2 * pairs if pairs == 2 else 1)
 
     def ghost_row(q, carry):
         ap = q // (ty + 2)
@@ -273,7 +312,7 @@
 
         @pl.when(jnp.logical_not(own) & held)
         def _():
-            source_row(ap, bp, list(range(tz + 2)))
+            source_row(ap, bp, list(range(tz + 2)), 2)
 
         return carry
 
@@ -319,13 +358,7 @@
         )
         right = jnp.concatenate(
             [
-                jnp.concatenate(
-                    [
-                        store[base + c, f, pl.ds(((ap - a) * 3 + bp - b) * 3 * tile, 3 * tile), :]
-                        for f in range(2)
-                    ],
-                    axis=1,
-                )
+                store[base + c, pl.ds(((ap - a) * 3 + bp - b) * 3 * tile, 3 * tile), :]
                 for ap, bp in pairs
             ],
             axis=0,
@@ -443,8 +476,8 @@
     for a, b, c in itertools.product(range(tx), range(ty), range(tz)):
         held = [basis[k, a + 1, b + 1, :, lanes(c + 1)] for k in range(ITERS)]
         held.append(last[a, b, :, lanes(c)])
-        sol_ref[:, a, b, c, :] = sum(x * v for x, v in zip(found, held))
-        res_ref[:, a, b, c, :] = sum(x * v for x, v in zip(rem, held))
+        out_ref[0, :, a, b, c, :] = sum(x * v for x, v in zip(found, held))
+        out_ref[1, :, a, b, c, :] = sum(x * v for x, v in zip(rem, held))
 
 
 def on_device(counts, positions, shield, width, hardness, softness, coupling, pair_bits, right_side):
@@ -452,26 +485,27 @@
     padded = (tx + 2, ty + 2)
     width_lanes = (tz + 2) * tile
     peers = counts[0] * counts[1] * counts[2]
-    field = jax.ShapeDtypeStruct((4, tx, ty, tz, tile), jnp.float32)
+    field = jax.ShapeDtypeStruct((2, 4, tx, ty, tz, tile), jnp.float32)
     vmem = pl.BlockSpec(memory_space=pltpu.VMEM)
-    return pl.pallas_call(
+    out = pl.pallas_call(
         functools.partial(kernel, counts, (tx, ty, tz), tile),
-        out_shape=(field, field),
+        out_shape=field,
         in_specs=[pl.BlockSpec(memory_space=pltpu.SMEM)] + [vmem] * 7,
-        out_specs=(vmem, vmem),
+        out_specs=vmem,
         scratch_shapes=[
-            pltpu.VMEM((tx * ty * tz, 2, 27 * tile, tile), jnp.bfloat16),
+            pltpu.VMEM((tx * ty * tz, 27 * tile, 2 * tile), jnp.bfloat16),
             pltpu.VMEM(padded + (8, width_lanes), jnp.float32),
             pltpu.VMEM((ITERS,) + padded + (4, width_lanes), jnp.float32),
             pltpu.VMEM((tx, ty, 4, tz * tile), jnp.float32),
             pltpu.VMEM((2,) + padded + (tz + 2, 16, tile), jnp.bfloat16),
             pltpu.VMEM((tz + 2, tile, 32), jnp.bfloat16),
-            pltpu.VMEM((tz + 2, tile, tile), jnp.float32),
-            pltpu.VMEM((tz + 2, tile, tile), jnp.float32),
+            pltpu.VMEM((tz + 2, tile, 2 * tile), jnp.float32),
+            pltpu.VMEM((32, 2 * tile), jnp.bfloat16),
+            pltpu.VMEM((2 * 3 * tz, tile, tile), jnp.float32),
             pltpu.VMEM((tx * ty * tz, 16, 2 * tile), jnp.float32),
             pltpu.VMEM((tx, ty, 4, tz * tile), jnp.float32),
-            pltpu.VMEM((2, 4, tile), jnp.float32),
-            pltpu.VMEM((2, peers, 4, tile), jnp.float32),
+            pltpu.VMEM((2, 1, tile), jnp.float32),
+            pltpu.VMEM((2, peers, 1, tile), jnp.float32),
             pltpu.SemaphoreType.DMA((ITERS + 1, 26)),
             pltpu.SemaphoreType.DMA((ITERS + 1, 26)),
             pltpu.SemaphoreType.DMA((2, peers)),
@@ -481,6 +515,7 @@
             collective_id=0, has_side_effects=True, vmem_limit_bytes=67043328
         ),
     )(pair_bits, positions, shield, width, hardness, softness, coupling, right_side)
+    return out[0], out[1]
 
 
 def solution(mesh):

time: 80.4 us -> 70.7 us (0.88)
  Pallas kernels: 77.4 us -> 68.3 us
    pallas_call x1, Pallas kernels: 77.4 us -> 68.3 us  [on_device(): pl.pallas_call(functools.partial(kernel, counts, (tx, ty, tz), tile), out...]
    unnamed x4 -> x0, local copies, waits for them, and re-layouts: 2.14 us -> none
    squeeze x0 -> x1, local copies, waits for them, and re-layouts: none -> 1.53 us  [on_device(): return (out[0], out[1])]
where the time goes in v3:
time: 70.7 us; the launch traced here: 70.5 us
  Pallas kernels  68.3 us (97%)
  local copies, waits for them, and re-layouts  1.53 us (2%)
    pallas_call x1, Pallas kernels, on_device(): pl.pallas_call(functools.partial(kernel, counts, (tx, ty, tz), tile), out...  68.3 us
    squeeze x1, local copies, waits for them, and re-layouts, on_device(): return (out[0], out[1])  1.53 us

profile of v3, /device:TPU:0, one launch (start us, length us, event | category | flops | bytes accessed | tf_op | source)
XLA Modules:
  0.0 70.5 jit_solution(2268617748046478477)
XLA Ops:
  0.6 68.3 %shard_map.95 = f32[2,4,2,2,8,128]{5,4,3,2,1,0:T(8,128)} custom-call(s32[2,2,8]{2,1,0:T(2,128)} %bits_ref.1, f32[3,2,2,8,128]{4,3,2,1,0:T(8,128)} %pos_ref.1, f32[2,2,8,128]{3,2,1,0:T(8,128)} %shield_ref.1, f32[2,2,8,128]{3,2,1,0:T(8,128)} %width_ref.1, f32[2,2,8,128]{3,2,1,0:T(8,128)} %hard_ref.1, f32[2,2,8,128]{3,2,1,0:T(8,128)} %soft_ref.1, ...), custom_call_target="tpu_custom_call" | custom-call | tf_op jit(solution)/shard_map/pallas_call | solution.py:490
  69.0 1.5 %slice_bitcast_fusion = (f32[4,2,2,8,128]{4,3,2,1,0:T(8,128)}, f32[4,2,2,8,128]{4,3,2,1,0:T(8,128)}) fusion(f32[2,4,2,2,8,128]{5,4,3,2,1,0:T(8,128)} %shard_map.95), kind=kLoop, calls=%fused_computation | loop fusion | bytes 262144 | tf_op jit(solution)/shard_map/squeeze | solution.py:518

commit v4 on v3

--- a/solution.py
+++ b/solution.py
@@ -433,12 +433,8 @@
         if k + 1 < ITERS:
             moments[2 * k + 2] = norm
             halo_start(basis.at[k + 1], 2 + k)
-        if k + 2 == ITERS:
-            sum_start(0, moments)
-            early, moments = list(moments), {}
-    sum_start(1, moments)
-    gram = sum_finish(0, early)
-    gram.update(sum_finish(1, list(moments)))
+    sum_start(0, moments)
+    gram = sum_finish(0, list(moments))
     gram = {n: jnp.broadcast_to(value, (4, tile)) for n, value in gram.items()}
 
     def dot(left, right):
@@ -504,12 +500,12 @@
             pltpu.VMEM((2 * 3 * tz, tile, tile), jnp.float32),
             pltpu.VMEM((tx * ty * tz, 16, 2 * tile), jnp.float32),
             pltpu.VMEM((tx, ty, 4, tz * tile), jnp.float32),
-            pltpu.VMEM((2, 1, tile), jnp.float32),
-            pltpu.VMEM((2, peers, 1, tile), jnp.float32),
+            pltpu.VMEM((1, 1, tile), jnp.float32),
+            pltpu.VMEM((1, peers, 1, tile), jnp.float32),
             pltpu.SemaphoreType.DMA((ITERS + 1, 26)),
             pltpu.SemaphoreType.DMA((ITERS + 1, 26)),
-            pltpu.SemaphoreType.DMA((2, peers)),
-            pltpu.SemaphoreType.DMA((2, peers)),
+            pltpu.SemaphoreType.DMA((1, peers)),
+            pltpu.SemaphoreType.DMA((1, peers)),
         ],
         compiler_params=pltpu.CompilerParams(
             collective_id=0, has_side_effects=True, vmem_limit_bytes=67043328

time: 70.7 us -> 70.2 us (level)
  no operation moved by 1% of the time
where the time goes in v4:
time: 70.2 us; the launch traced here: 69.9 us
  Pallas kernels  67.8 us (97%)
  local copies, waits for them, and re-layouts  1.53 us (2%)
    pallas_call x1, Pallas kernels, on_device(): pl.pallas_call(functools.partial(kernel, counts, (tx, ty, tz), tile), out...  67.8 us
    squeeze x1, local copies, waits for them, and re-layouts, on_device(): return (out[0], out[1])  1.53 us

profile of v4, /device:TPU:0, one launch (start us, length us, event | category | flops | bytes accessed | tf_op | source)
XLA Modules:
  0.0 69.9 jit_solution(7086993386247858547)
XLA Ops:
  0.6 67.8 %shard_map.95 = f32[2,4,2,2,8,128]{5,4,3,2,1,0:T(8,128)} custom-call(s32[2,2,8]{2,1,0:T(2,128)} %bits_ref.1, f32[3,2,2,8,128]{4,3,2,1,0:T(8,128)} %pos_ref.1, f32[2,2,8,128]{3,2,1,0:T(8,128)} %shield_ref.1, f32[2,2,8,128]{3,2,1,0:T(8,128)} %width_ref.1, f32[2,2,8,128]{3,2,1,0:T(8,128)} %hard_ref.1, f32[2,2,8,128]{3,2,1,0:T(8,128)} %soft_ref.1, ...), custom_call_target="tpu_custom_call" | custom-call | tf_op jit(solution)/shard_map/pallas_call | solution.py:486
  68.4 1.5 %slice_bitcast_fusion = (f32[4,2,2,8,128]{4,3,2,1,0:T(8,128)}, f32[4,2,2,8,128]{4,3,2,1,0:T(8,128)}) fusion(f32[2,4,2,2,8,128]{5,4,3,2,1,0:T(8,128)} %shard_map.95), kind=kLoop, calls=%fused_computation | loop fusion | bytes 262144 | tf_op jit(solution)/shard_map/squeeze | solution.py:514
